TPU v7x, 32 devices: a whole 2x2x4 slice. The times are simulated.
32 devices in a mesh: band: 32 (over z, y, x, core).
Axes of the slice: x: 2, y: 2, z: 4, core: 2. Of those that a mesh axis runs over, the one named last changes fastest.
Arguments:
- jones_start: float32 [32, 32, 512], P('band'), may hold values from -1.5 to 1.5
- visible: bfloat16 [32, 8, 4096], P('band'), may hold values from -6 to 6
- coherent: bfloat16 [32, 32, 4096], P('band'), may hold values from -1 to 1
- stations: int32 [2, 4096], replicated, may hold values from 0 to 511, as said below
- weights: float32 [32, 512], P('band'), may hold values from 0.2 to 2
- multiplier_start: float32 [32, 32, 512], P('band'), may hold values from -2 to 2
Outputs:
- jones_final: float32 [32, 32, 512], P('band')
- multiplier_final: float32 [32, 32, 512], P('band')
- coefficients: float32 [96, 512], P(None, 'band')
Inputs may be any that keep to these rules, and one draw needn't show every extreme that they name: Rows 0 and 1 of each column name two different stations; the same baselines serve every subband.
All inputs are finite; a program needn't handle non-finite values.
Results may differ from a plain program's by a relative error of at most 0.0003.
Values sent between devices are 32-bit elements; how exact they have to be, the bound alone decides.
A program may use at most 64 MiB of HBM per device.

v0:
```python
import jax
import jax.numpy as jnp
from jax import lax
from jax.sharding import PartitionSpec as P

ITERS = 2
PENALTY = 1.0
STEP_SIZE = 0.05
PAIR_LIST = ((0, 0), (0, 1), (0, 2), (1, 1), (1, 2), (2, 2))


def matrix_product(first_real, first_imag, second_real, second_imag):

    def contract(lhs_part, rhs_part):
        return jnp.sum(lhs_part[:, :, :, None, :] * rhs_part[:, None, :, :, :], axis=2)

    real_part = contract(first_real, second_real) - contract(first_imag, second_imag)
    imag_part = contract(first_real, second_imag) + contract(first_imag, second_real)
    return (real_part, imag_part)


def band_loss(
    jones_band, visible_band, coherent_band, stations, target_band, multiplier_band, weight_band
):
    baseline_count = stations.shape[1]
    direction_count = jones_band.shape[0] // 8
    station_first = jnp.take(jones_band, stations[0], axis=1).reshape(
        direction_count, 2, 2, 2, baseline_count
    )
    station_second = jnp.take(jones_band, stations[1], axis=1).reshape(
        direction_count, 2, 2, 2, baseline_count
    )
    sky_model = coherent_band.astype(jnp.float32).reshape(direction_count, 2, 2, 2, baseline_count)
    inner_real, inner_imag = matrix_product(
        station_first[:, 0], station_first[:, 1], sky_model[:, 0], sky_model[:, 1]
    )
    herm_real = jnp.swapaxes(station_second[:, 0], 1, 2)
    herm_imag = -jnp.swapaxes(station_second[:, 1], 1, 2)
    model_real, model_imag = matrix_product(inner_real, inner_imag, herm_real, herm_imag)
    predicted = jnp.stack([jnp.sum(model_real, axis=0), jnp.sum(model_imag, axis=0)])
    misfit = visible_band.astype(jnp.float32).reshape(2, 2, 2, baseline_count) - predicted
    data_scale = jones_band.shape[1] / (2.0 * baseline_count)
    distance = jones_band - target_band
    return (
        data_scale * jnp.sum(misfit * misfit)
        + jnp.sum(multiplier_band * distance)
        + 0.5 * PENALTY * jnp.sum(weight_band[None, :] * distance * distance)
    )


def descend(
    jones_band, visible_band, coherent_band, stations, target_band, multiplier_band, weight_band
):
    slope_fn = jax.grad(band_loss)
    slope = slope_fn(
        jones_band, visible_band, coherent_band, stations, target_band, multiplier_band, weight_band
    )
    jones_band = jones_band - STEP_SIZE * slope
    return jones_band


def solve_normal(normal_matrix, right_side):
    gram_aa, gram_ab, gram_ac, gram_bb, gram_bc, gram_cc = [
        normal_matrix[position] for position in range(6)
    ]
    cofac_aa = gram_bb * gram_cc - gram_bc * gram_bc
    cofac_ab = gram_ac * gram_bc - gram_ab * gram_cc
    cofac_ac = gram_ab * gram_bc - gram_ac * gram_bb
    cofac_bb = gram_aa * gram_cc - gram_ac * gram_ac
    cofac_bc = gram_ab * gram_ac - gram_aa * gram_bc
    cofac_cc = gram_aa * gram_bb - gram_ab * gram_ab
    determinant = gram_aa * cofac_aa + gram_ab * cofac_ab + gram_ac * cofac_ac
    inverse_det = 1.0 / determinant
    first_term = right_side[0]
    second_term = right_side[1]
    third_term = right_side[2]
    coeff_a = (cofac_aa * first_term + cofac_ab * second_term + cofac_ac * third_term) * inverse_det
    coeff_b = (cofac_ab * first_term + cofac_bb * second_term + cofac_bc * third_term) * inverse_det
    coeff_c = (cofac_ac * first_term + cofac_bc * second_term + cofac_cc * third_term) * inverse_det
    return jnp.stack([coeff_a, coeff_b, coeff_c])


def local(jones_start, visible, coherent, stations, weights, multiplier_start):
    band_count = lax.axis_size("band")
    band_index = lax.axis_index("band")
    abscissa = -1.0 + 2.0 * band_index.astype(jnp.float32) / (band_count - 1)
    basis_local = (jnp.ones((), jnp.float32), abscissa, 1.5 * abscissa * abscissa - 0.5)
    weight_band = weights[0]
    visible_band = visible[0]
    coherent_band = coherent[0]
    station_share = weights.shape[1] // band_count
    products = jnp.stack(
        [basis_local[first_idx] * basis_local[second_idx] for first_idx, second_idx in PAIR_LIST]
    )
    normal_term = PENALTY * products[:, None] * weight_band[None, :]
    normal_solver = lax.psum(normal_term, "band")

    def iteration(turn_index, carried):
        jones_band, multiplier_band, owned_prior = carried
        combined = multiplier_band + PENALTY * weight_band[None, :] * jones_band
        weighted_terms = jnp.stack([basis_local[term_index] * combined for term_index in range(3)])
        full_sums = lax.psum(weighted_terms, "band")
        coefficients = solve_normal(normal_solver, full_sums)
        owned_coeff = lax.dynamic_slice_in_dim(
            coefficients, band_index * station_share, station_share, 2
        )
        target_band = (
            basis_local[0] * coefficients[0]
            + basis_local[1] * coefficients[1]
            + basis_local[2] * coefficients[2]
        )
        multiplier_band = multiplier_band + PENALTY * weight_band[None, :] * (
            jones_band - target_band
        )
        jones_band = descend(
            jones_band,
            visible_band,
            coherent_band,
            stations,
            target_band,
            multiplier_band,
            weight_band,
        )
        return (jones_band, multiplier_band, owned_coeff)

    owned_start = jnp.zeros((3, jones_start.shape[1], station_share), jnp.float32)
    jones_band, multiplier_band, owned_coeff = lax.fori_loop(
        0, ITERS, iteration, (jones_start[0], multiplier_start[0], owned_start)
    )
    coeff_rows = owned_coeff.reshape(
        owned_coeff.shape[0] * owned_coeff.shape[1], owned_coeff.shape[2]
    )
    return (jones_band[None], multiplier_band[None], coeff_rows)


def solution(mesh):
    return jax.shard_map(
        local,
        mesh=mesh,
        in_specs=(
            P("band", None, None),
            P("band", None, None),
            P("band", None, None),
            P(),
            P("band", None),
            P("band", None, None),
        ),
        out_specs=(P("band", None, None), P("band", None, None), P(None, "band")),
        check_vma=False,
    )
```

profile of v0, /device:TPU:8, one launch (start us, length us, event | category | flops | bytes accessed | tf_op | source)
XLA Modules:
  0.0 373.0 jit_solution(7236217893154198396)
XLA Ops:
  7.2 0.8 copy.133
  8.0 0.8 copy.134
  8.9 0.8 broadcast_multiply_fusion.1
  9.7 40.5 %psum.17 = f32[6,512]{1,0:T(8,128)S(1)} all-reduce(f32[6,512]{1,0:T(8,128)S(1)} %broadcast_multiply_fusion.1), channel_id=1, replica_groups=mesh['band'=32] {'band'}, use_global_device_ids=true, to_apply=%region_0.0 | all-reduce | flops 3072 | bytes 24576 | tf_op jit(solution)/shard_map/psum | solution.py:96
  50.1 0.6 multiply_add_fusion.2
  50.8 313.9 %while.17 = (s32[]{:T(128)}, f32[32,512]{1,0:T(8,128)S(1)}, f32[32,512]{1,0:T(8,128)S(1)}, f32[3,32,16]{2,1,0:T(8,128)}, f32[1,512]{1,0:T(1,128)}, /*index=5*/f3...) while((s32[]{:T(128)}, f32[32,512]{1,0:T(8,128)S(1)}, ...), condition=%wide.region_27.0_spmd, body=%wide.region_1.28_spmd.sunk | while | flops 6967298 | bytes 52347996 | solution.py:127
  50.8 0.7 multiply_bitcast_fusion.4
  51.5 0.7 pad_maximum_fusion.2
  52.3 0.9 fusion.32
  53.2 0.6 compare_select_fusion.3
  53.8 14.1 %gather_fusion.1 = f32[4096,32]{1,0:T(8,128)} fusion(f32[32,512]{0,1:T(8,128)S(1)} %copy.101, s32[4096]{0:T(1024)S(1)} %get-tuple-element.581), kind=kCustom, calls=%fused_computation.1.clone.clone.1 | custom fusion | bytes 1064960 | tf_op jit(solution)/shard_map/while/body/eval_jaxpr/jvp(jit(_take))/gather | solution.py:27
  67.9 3.6 select_bitcast_fusion.5
  71.5 0.6 copy.105
  72.5 0.9 copy.106
  73.4 0.9 copy.108
  74.3 0.3 reshape.303
  75.0 14.1 %gather_fusion = f32[4096,32]{1,0:T(8,128)} fusion(f32[32,512]{0,1:T(8,128)S(1)} %copy.101, s32[4096]{0:T(1024)S(1)} %get-tuple-element.578), kind=kCustom, calls=%fused_computation.clone.clone.1 | custom fusion | bytes 1064960 | tf_op jit(solution)/shard_map/while/body/eval_jaxpr/jvp(jit(_take))/gather | solution.py:30
  89.1 3.6 select_bitcast_fusion.4
  92.7 0.6 copy.103
  94.4 0.6 multiply_reduce_fusion.24
  95.2 0.6 multiply_reduce_fusion.25
  95.8 0.5 add_reduce_fusion.2
  96.4 1.3 multiply_reduce_fusion.26
  97.9 0.6 multiply_reduce_fusion.27
  99.3 0.4 copy.113
  99.7 0.4 reshape.305
  100.1 2.0 copy.114
  102.0 0.4 copy.111
  102.5 0.4 reshape.304
  102.9 0.6 copy.112
  103.5 22.7 %scatter_custom_fusion.8 = f32[32,512]{0,1:T(8,128)S(1)} fusion(s32[4096]{0:T(1024)} %get-tuple-element.603, f32[4096,32]{1,0:T(8,128)} %copy.114, f32[]{:T(128)} %constant.70.clone.25..sunk), kind=kCustom, calls=%fused_computation.50.clone.1 | custom fusion | flops 131072 | bytes 66048 | tf_op jit(solution)/shard_map/while/body/eval_jaxpr/transpose(jvp(jit(_take)))/scatter-add | solution.py:27
  126.2 57.3 %all-reduce.6.cloned.1.call-done = f32[3,32,512]{2,1,0:T(8,128)} async-done(((f32[3,32,512]{2,1,0:T(8,128)}), f32[3,32,512]{2,1,0:T(8,128)}) %all-reduce.6.cloned.1.call-update) | async-done | bytes 196624 | tf_op jit(solution)/shard_map/while/body/eval_jaxpr/psum | solution.py:102
  183.5 1.0 add_add_fusion.2
  184.7 22.5 %scatter_fusion = f32[32,512]{0,1:T(8,128)S(1)} fusion(f32[32,512]{0,1:T(8,128)S(1)} %copy.102, s32[4096]{0:T(1024)S(1)} %get-tuple-element.577, f32[4096,32]{1,0:T(8,128)S(1)} %copy.112), kind=kCustom, calls=%fused_computation.2.clone.1 | custom fusion | flops 131072 | bytes 1589248 | tf_op jit(solution)/shard_map/while/body/eval_jaxpr/transpose(jvp(jit(_take)))/scatter-add | solution.py:30
  207.4 0.7 fusion.36
  208.1 0.7 multiply_bitcast_fusion.4
  208.8 0.7 pad_maximum_fusion.2
  209.6 0.9 fusion.32
  210.5 0.6 compare_select_fusion.3
  211.2 14.1 %gather_fusion.1 = f32[4096,32]{1,0:T(8,128)} fusion(f32[32,512]{0,1:T(8,128)S(1)} %copy.101, s32[4096]{0:T(1024)S(1)} %get-tuple-element.581), kind=kCustom, calls=%fused_computation.1.clone.clone.1 | custom fusion | bytes 1064960 | tf_op jit(solution)/shard_map/while/body/eval_jaxpr/jvp(jit(_take))/gather | solution.py:27
  225.3 3.6 select_bitcast_fusion.5
  228.9 0.6 copy.105
  229.8 0.9 copy.106
  230.7 0.9 copy.108
  232.3 14.1 %gather_fusion = f32[4096,32]{1,0:T(8,128)} fusion(f32[32,512]{0,1:T(8,128)S(1)} %copy.101, s32[4096]{0:T(1024)S(1)} %get-tuple-element.578), kind=kCustom, calls=%fused_computation.clone.clone.1 | custom fusion | bytes 1064960 | tf_op jit(solution)/shard_map/while/body/eval_jaxpr/jvp(jit(_take))/gather | solution.py:30
  246.4 3.6 select_bitcast_fusion.4
  250.0 0.6 copy.103
  251.7 0.6 multiply_reduce_fusion.24
  252.5 0.6 multiply_reduce_fusion.25
  253.1 0.5 add_reduce_fusion.2
  253.8 1.3 multiply_reduce_fusion.26
  255.2 0.6 multiply_reduce_fusion.27
  256.6 0.4 copy.113
  257.0 0.4 reshape.305
  257.4 2.0 copy.114
  259.4 0.4 copy.111
  259.8 0.4 reshape.304
  260.2 0.6 copy.112
  260.8 22.7 %scatter_custom_fusion.8 = f32[32,512]{0,1:T(8,128)S(1)} fusion(s32[4096]{0:T(1024)} %get-tuple-element.603, f32[4096,32]{1,0:T(8,128)} %copy.114, f32[]{:T(128)} %constant.70.clone.25..sunk), kind=kCustom, calls=%fused_computation.50.clone.1 | custom fusion | flops 131072 | bytes 66048 | tf_op jit(solution)/shard_map/while/body/eval_jaxpr/transpose(jvp(jit(_take)))/scatter-add | solution.py:27
  283.5 56.6 %all-reduce.6.cloned.1.call-done = f32[3,32,512]{2,1,0:T(8,128)} async-done(((f32[3,32,512]{2,1,0:T(8,128)}), f32[3,32,512]{2,1,0:T(8,128)}) %all-reduce.6.cloned.1.call-update) | async-done | bytes 196624 | tf_op jit(solution)/shard_map/while/body/eval_jaxpr/psum | solution.py:102
  340.1 1.0 add_add_fusion.2
  341.3 22.5 %scatter_fusion = f32[32,512]{0,1:T(8,128)S(1)} fusion(f32[32,512]{0,1:T(8,128)S(1)} %copy.102, s32[4096]{0:T(1024)S(1)} %get-tuple-element.577, f32[4096,32]{1,0:T(8,128)S(1)} %copy.112), kind=kCustom, calls=%fused_computation.2.clone.1 | custom fusion | flops 131072 | bytes 1589248 | tf_op jit(solution)/shard_map/while/body/eval_jaxpr/transpose(jvp(jit(_take)))/scatter-add | solution.py:30
  364.0 0.7 fusion.36
  364.7 1.5 copy.85
  (131 shorter events, 7.3 us)
Async XLA Ops:
  50.8 132.8 %all-reduce.6.cloned.1.call-start = ((), (), s32[]{:S(2)}) async-start(), calls=%async_computation | async-start | bytes 393216 | tf_op jit(solution)/shard_map/while/body/eval_jaxpr/psum | solution.py:102
  72.1 2.1 copy-start.5
  93.3 0.8 copy-start.6
  93.3 1.0 copy-start
  93.3 1.1 copy-start.1
  95.1 1.3 copy-start.7
  98.6 0.7 copy-start.14
  102.4 81.1 %copy-start.8 = (f32[1,512]{1,0:T(1,128)S(1)}, f32[1,512]{1,0:T(1,128)}, u32[]{:S(2)}) copy-start(f32[1,512]{1,0:T(1,128)} %get-tuple-element.667) | copy-start | bytes 6148 | tf_op jit(solution)/shard_map/while
  102.4 81.1 %copy-start.9 = (f32[1,512]{1,0:T(1,128)S(1)}, f32[1,512]{1,0:T(1,128)}, u32[]{:S(2)}) copy-start(f32[1,512]{1,0:T(1,128)} %get-tuple-element.666) | copy-start | bytes 6148 | tf_op jit(solution)/shard_map/while
  102.4 81.1 %copy-start.10 = (f32[1,512]{1,0:T(1,128)S(1)}, f32[1,512]{1,0:T(1,128)}, u32[]{:S(2)}) copy-start(f32[1,512]{1,0:T(1,128)} %get-tuple-element.663) | copy-start | bytes 6148 | tf_op jit(solution)/shard_map/while
  102.5 81.1 %copy-start.11 = (f32[1,512]{1,0:T(1,128)S(1)}, f32[1,512]{1,0:T(1,128)}, u32[]{:S(2)}) copy-start(f32[1,512]{1,0:T(1,128)} %get-tuple-element.671) | copy-start | bytes 6148 | tf_op jit(solution)/shard_map/while
  102.5 81.1 %copy-start.12 = (f32[1,512]{1,0:T(1,128)S(1)}, f32[1,512]{1,0:T(1,128)}, u32[]{:S(2)}) copy-start(f32[1,512]{1,0:T(1,128)} %get-tuple-element.670) | copy-start | bytes 6148 | tf_op jit(solution)/shard_map/while
  102.5 81.1 %copy-start.13 = (f32[1,512]{1,0:T(1,128)S(1)}, f32[1,512]{1,0:T(1,128)}, u32[]{:S(2)}) copy-start(f32[1,512]{1,0:T(1,128)} %get-tuple-element.669) | copy-start | bytes 6148 | tf_op jit(solution)/shard_map/while
  184.7 22.7 %copy-start.2 = (f32[3,32,512]{2,1,0:T(8,128)S(1)}, f32[3,32,512]{2,1,0:T(8,128)}, u32[]{:S(2)}) copy-start(f32[3,32,512]{2,1,0:T(8,128)} %all-reduce.6.cloned.1.call-done) | copy-start | bytes 589828 | tf_op jit(solution)/shard_map/while
  208.1 132.0 %all-reduce.6.cloned.1.call-start = ((), (), s32[]{:S(2)}) async-start(), calls=%async_computation | async-start | bytes 393216 | tf_op jit(solution)/shard_map/while/body/eval_jaxpr/psum | solution.py:102
  229.4 2.1 copy-start.5
  250.6 0.8 copy-start.6
  250.6 1.0 copy-start
  250.6 1.1 copy-start.1
  252.5 1.3 copy-start.7
  255.9 0.7 copy-start.14
  259.8 80.3 %copy-start.8 = (f32[1,512]{1,0:T(1,128)S(1)}, f32[1,512]{1,0:T(1,128)}, u32[]{:S(2)}) copy-start(f32[1,512]{1,0:T(1,128)} %get-tuple-element.667) | copy-start | bytes 6148 | tf_op jit(solution)/shard_map/while
  259.8 80.3 %copy-start.9 = (f32[1,512]{1,0:T(1,128)S(1)}, f32[1,512]{1,0:T(1,128)}, u32[]{:S(2)}) copy-start(f32[1,512]{1,0:T(1,128)} %get-tuple-element.666) | copy-start | bytes 6148 | tf_op jit(solution)/shard_map/while
  259.8 80.3 %copy-start.10 = (f32[1,512]{1,0:T(1,128)S(1)}, f32[1,512]{1,0:T(1,128)}, u32[]{:S(2)}) copy-start(f32[1,512]{1,0:T(1,128)} %get-tuple-element.663) | copy-start | bytes 6148 | tf_op jit(solution)/shard_map/while
  259.8 80.3 %copy-start.11 = (f32[1,512]{1,0:T(1,128)S(1)}, f32[1,512]{1,0:T(1,128)}, u32[]{:S(2)}) copy-start(f32[1,512]{1,0:T(1,128)} %get-tuple-element.671) | copy-start | bytes 6148 | tf_op jit(solution)/shard_map/while
  259.8 80.3 %copy-start.12 = (f32[1,512]{1,0:T(1,128)S(1)}, f32[1,512]{1,0:T(1,128)}, u32[]{:S(2)}) copy-start(f32[1,512]{1,0:T(1,128)} %get-tuple-element.670) | copy-start | bytes 6148 | tf_op jit(solution)/shard_map/while
  259.8 80.3 %copy-start.13 = (f32[1,512]{1,0:T(1,128)S(1)}, f32[1,512]{1,0:T(1,128)}, u32[]{:S(2)}) copy-start(f32[1,512]{1,0:T(1,128)} %get-tuple-element.669) | copy-start | bytes 6148 | tf_op jit(solution)/shard_map/while
  341.3 22.7 %copy-start.2 = (f32[3,32,512]{2,1,0:T(8,128)S(1)}, f32[3,32,512]{2,1,0:T(8,128)}, u32[]{:S(2)}) copy-start(f32[3,32,512]{2,1,0:T(8,128)} %all-reduce.6.cloned.1.call-done) | copy-start | bytes 589828 | tf_op jit(solution)/shard_map/while
  364.7 1.5 copy-start.3
  364.7 1.5 copy-start.4
Sparse Core Ops, SparseCore 0:
  57.1 126.3 all-reduce.5
  214.4 125.6 all-reduce.5
where the time goes:
time: 374 us; the launch traced here: 373 us
  other arithmetic  123 us (33%)
  waiting for transfers between devices  114 us (30%)
  local copies, waits for them, and re-layouts  80.8 us (22%)
  blocking collectives  40.5 us (11%)
  between operations  14 us (4%)
    psum x2, waiting for transfers between devices, iteration(): full_sums = lax.psum(weighted_terms, 'band')  114 us
    scatter-add x2, other arithmetic, band_loss(): jnp.take(jones_band, stations[0], axis=1)  45.4 us
    scatter-add x2, other arithmetic, band_loss(): jnp.take(jones_band, stations[1], axis=1)  45 us
    psum x1, blocking collectives, local(): normal_solver = lax.psum(normal_term, 'band')  40.5 us
    gather x2, local copies, waits for them, and re-layouts, band_loss(): jnp.take(jones_band, stations[0], axis=1)  28.2 us
    gather x2, local copies, waits for them, and re-layouts, band_loss(): jnp.take(jones_band, stations[1], axis=1)  28.2 us
    select_n x4, other arithmetic, band_loss(): jnp.take(jones_band, stations[0], axis=1)  8.44 us
  transfers between devices with their start and end apart: 2, of which 2 were waited for; matrix products, arithmetic and copies ran while one was open for 39% of the time, Pallas kernels for 0%

commit v1 on v0

--- a/solution.py
+++ b/solution.py
@@ -7,6 +7,15 @@
 PENALTY = 1.0
 STEP_SIZE = 0.05
 PAIR_LIST = ((0, 0), (0, 1), (0, 2), (1, 1), (1, 2), (2, 2))
+
+
+def add_in_pairs(value, mesh_axis):
+    n_dev = lax.axis_size(mesh_axis)
+    summed, stride = (value, 1)
+    while stride < n_dev:
+        summed = summed + lax.ppermute(summed, mesh_axis, [(i, i ^ stride) for i in range(n_dev)])
+        stride = 2 * stride
+    return summed
 
 
 def matrix_product(first_real, first_imag, second_real, second_imag):
@@ -99,7 +108,7 @@
         jones_band, multiplier_band, owned_prior = carried
         combined = multiplier_band + PENALTY * weight_band[None, :] * jones_band
         weighted_terms = jnp.stack([basis_local[term_index] * combined for term_index in range(3)])
-        full_sums = lax.psum(weighted_terms, "band")
+        full_sums = add_in_pairs(weighted_terms, "band")
         coefficients = solve_normal(normal_solver, full_sums)
         owned_coeff = lax.dynamic_slice_in_dim(
             coefficients, band_index * station_share, station_share, 2

time: 374 us -> 310 us (0.83); the launches traced: 373 us -> 305 us
  waiting for transfers between devices: 114 us -> 36.4 us
  between operations: 14 us -> 0.63 us
  starting transfers between devices: 0.01 us -> 12.8 us
  other arithmetic: 123 us -> 128 us
  local copies, waits for them, and re-layouts: 80.8 us -> 85.2 us
    psum x2 -> x0, waiting for transfers between devices: 114 us -> none  [iteration(): full_sums = lax.psum(weighted_terms, 'band')]
    ppermute x0 -> x10, waiting for transfers between devices: none -> 36.4 us  [add_in_pairs(): lax.ppermute(summed, mesh_axis, [(i, i ^ stride) for i in range(n_dev)])]
    ppermute x0 -> x10, starting transfers between devices: none -> 12.8 us  [add_in_pairs(): lax.ppermute(summed, mesh_axis, [(i, i ^ stride) for i in range(n_dev)])]
    add x0 -> x10, other arithmetic: none -> 4.02 us  [add_in_pairs(): summed + lax.ppermute(summed, mesh_axis, [(i, i ^ stride) for i in range(...]
  transfers between devices with their start and end apart: 2 -> 10, of which waited for: 2 -> 6; matrix products, arithmetic and copies ran while one was open for 39% -> 48% of each run, Pallas kernels for 0% -> 0%
where the time goes in v1:
time: 310 us; the launch traced here: 305 us
  other arithmetic  128 us (41%)
  local copies, waits for them, and re-layouts  85.2 us (27%)
  blocking collectives  40.5 us (13%)
  waiting for transfers between devices  36.4 us (12%)
  starting transfers between devices  12.8 us (4%)
    scatter-add x2, other arithmetic, band_loss(): jnp.take(jones_band, stations[0], axis=1)  45.4 us
    scatter-add x2, other arithmetic, band_loss(): jnp.take(jones_band, stations[1], axis=1)  45 us
    psum x1, blocking collectives, local(): normal_solver = lax.psum(normal_term, 'band')  40.5 us
    ppermute x10, waiting for transfers between devices, add_in_pairs(): lax.ppermute(summed, mesh_axis, [(i, i ^ stride) for i in range(n_dev)])  36.4 us
    gather x2, local copies, waits for them, and re-layouts, band_loss(): jnp.take(jones_band, stations[0], axis=1)  28.2 us
    gather x2, local copies, waits for them, and re-layouts, band_loss(): jnp.take(jones_band, stations[1], axis=1)  28.2 us
    ppermute x10, starting transfers between devices, add_in_pairs(): lax.ppermute(summed, mesh_axis, [(i, i ^ stride) for i in range(n_dev)])  12.8 us
    select_n x4, other arithmetic, band_loss(): jnp.take(jones_band, stations[0], axis=1)  8.41 us
  transfers between devices with their start and end apart: 10, of which 6 were waited for; matrix products, arithmetic and copies ran while one was open for 48% of the time, Pallas kernels for 0%

profile of v1, /device:TPU:8, one launch (start us, length us, event | category | flops | bytes accessed | tf_op | source)
XLA Modules:
  0.0 305.1 jit_solution(10061512193636918298)
XLA Ops:
  0.6 1.5 copy.151
  2.1 1.5 copy.152
  3.7 0.8 broadcast_multiply_fusion.1
  4.4 40.5 %psum.7 = f32[6,512]{1,0:T(8,128)S(1)} all-reduce(f32[6,512]{1,0:T(8,128)S(1)} %broadcast_multiply_fusion.1), channel_id=1, replica_groups=mesh['band'=32] {'band'}, use_global_device_ids=true, to_apply=%region_0.0 | all-reduce | flops 3072 | bytes 24576 | tf_op jit(solution)/shard_map/psum | solution.py:105
  44.9 0.6 multiply_add_fusion.2
  45.5 258.1 %while.17 = (s32[]{:T(128)}, f32[32,512]{1,0:T(8,128)}, f32[32,512]{1,0:T(8,128)}, f32[3,32,16]{2,1,0:T(8,128)}, f32[1,512]{1,0:T(1,128)}, /*index=5*/f32[1,512]...) while((s32[]{:T(128)}, f32[32,512]{1,0:T(8,128)}, ...), condition=%wide.region_26.0_spmd, body=%wide.region_1.27_spmd.sunk | while | flops 7409666 | bytes 57984280 | solution.py:136
  45.5 0.9 multiply_bitcast_fusion.4
  46.4 0.7 pad_maximum_fusion.2
  47.1 1.0 copy.120
  48.1 0.9 fusion.38
  49.6 14.1 %gather_fusion.1 = f32[4096,32]{1,0:T(8,128)} fusion(f32[32,512]{0,1:T(8,128)S(1)} %copy.120, s32[4096]{0:T(1024)S(1)} %get-tuple-element.581), kind=kCustom, calls=%fused_computation.1.clone.clone.1 | custom fusion | bytes 1064960 | tf_op jit(solution)/shard_map/while/body/eval_jaxpr/jvp(jit(_take))/gather | solution.py:36
  63.7 3.6 %select_bitcast_fusion.5 = f32[32,4096]{0,1:T(8,128)S(1)} fusion(f32[4096,32]{1,0:T(8,128)} %gather_fusion.1, pred[4096]{0:T(1024)(128)(4,1)S(1)} %compare_and_fusion.5), kind=kLoop, calls=%fused_computation.4.clone.1 | loop fusion | flops 131072 | bytes 1052672 | tf_op jit(solution)/shard_map/while/body/eval_jaxpr/jvp(jit(_take))/select_n | solution.py:36
  68.2 0.9 copy.125
  69.1 0.9 copy.127
  70.8 14.1 %gather_fusion = f32[4096,32]{1,0:T(8,128)} fusion(f32[32,512]{0,1:T(8,128)S(1)} %copy.120, s32[4096]{0:T(1024)S(1)} %get-tuple-element.578), kind=kCustom, calls=%fused_computation.clone.clone.1 | custom fusion | bytes 1064960 | tf_op jit(solution)/shard_map/while/body/eval_jaxpr/jvp(jit(_take))/gather | solution.py:39
  84.9 3.6 %select_bitcast_fusion.4 = f32[32,4096]{0,1:T(8,128)S(1)} fusion(f32[4096,32]{1,0:T(8,128)} %gather_fusion, pred[4096]{0:T(1024)(128)(4,1)S(1)} %compare_and_fusion.4), kind=kLoop, calls=%fused_computation.5.clone.1 | loop fusion | flops 131072 | bytes 1052672 | tf_op jit(solution)/shard_map/while/body/eval_jaxpr/jvp(jit(_take))/select_n | solution.py:39
  90.1 0.6 multiply_reduce_fusion.24
  90.9 0.6 multiply_reduce_fusion.25
  92.2 1.3 multiply_reduce_fusion.26
  93.6 0.6 multiply_reduce_fusion.27
  95.1 1.0 fusion.36
  96.0 2.3 collective-permute-start.1
  98.4 5.5 %collective-permute-done.1 = f32[3,32,512]{2,1,0:T(8,128)S(1)} collective-permute-done((f32[3,32,512]{2,1,0:T(8,128)S(1)}, f32[3,32,512]{2,1,0:T(8,128)S(1)}, u32[]{:S(2)}, u32[]{:S(2)}) %collective-permute-start.1) | collective-permute-done | bytes 196640 | tf_op jit(solution)/shard_map/while/body/eval_jaxpr/ppermute | solution.py:16
  103.9 1.0 fusion.37
  104.9 1.8 collective-permute-start.2
  107.6 2.0 copy.133
  111.0 22.7 %scatter_custom_fusion.8 = f32[32,512]{0,1:T(8,128)S(1)} fusion(s32[4096]{0:T(1024)} %get-tuple-element.603, f32[4096,32]{1,0:T(8,128)} %copy.133, f32[]{:T(128)} %constant.70.clone.25..sunk), kind=kCustom, calls=%fused_computation.50.clone.1 | custom fusion | flops 131072 | bytes 66048 | tf_op jit(solution)/shard_map/while/body/eval_jaxpr/transpose(jvp(jit(_take)))/scatter-add | solution.py:36
  134.4 5.6 %collective-permute-done.3 = f32[3,32,512]{2,1,0:T(8,128)S(1)} collective-permute-done((f32[3,32,512]{2,1,0:T(8,128)S(1)}, f32[3,32,512]{2,1,0:T(8,128)S(1)}, u32[]{:S(2)}, u32[]{:S(2)}) %collective-permute-start.3) | collective-permute-done | bytes 196640 | tf_op jit(solution)/shard_map/while/body/eval_jaxpr/ppermute | solution.py:16
  140.0 1.3 collective-permute-start.4
  141.4 7.0 %collective-permute-done.4 = f32[3,32,512]{2,1,0:T(8,128)S(1)} collective-permute-done((f32[3,32,512]{2,1,0:T(8,128)S(1)}, f32[3,32,512]{2,1,0:T(8,128)S(1)}, u32[]{:S(2)}, u32[]{:S(2)}) %collective-permute-start.4) | collective-permute-done | bytes 196640 | tf_op jit(solution)/shard_map/while/body/eval_jaxpr/ppermute | solution.py:16
  148.6 1.6 add_add_fusion.2
  150.3 22.5 %scatter_fusion = f32[32,512]{0,1:T(8,128)S(1)} fusion(f32[32,512]{0,1:T(8,128)S(1)} %copy.121, s32[4096]{0:T(1024)S(1)} %get-tuple-element.577, f32[4096,32]{1,0:T(8,128)S(1)} %copy.131), kind=kCustom, calls=%fused_computation.2.clone.1 | custom fusion | flops 131072 | bytes 1589248 | tf_op jit(solution)/shard_map/while/body/eval_jaxpr/transpose(jvp(jit(_take)))/scatter-add | solution.py:39
  172.8 0.7 copy.134
  173.6 0.7 fusion.42
  174.3 0.9 multiply_bitcast_fusion.4
  175.2 0.7 pad_maximum_fusion.2
  175.9 1.0 copy.120
  176.8 0.9 fusion.38
  178.4 14.1 %gather_fusion.1 = f32[4096,32]{1,0:T(8,128)} fusion(f32[32,512]{0,1:T(8,128)S(1)} %copy.120, s32[4096]{0:T(1024)S(1)} %get-tuple-element.581), kind=kCustom, calls=%fused_computation.1.clone.clone.1 | custom fusion | bytes 1064960 | tf_op jit(solution)/shard_map/while/body/eval_jaxpr/jvp(jit(_take))/gather | solution.py:36
  192.4 3.6 %select_bitcast_fusion.5 = f32[32,4096]{0,1:T(8,128)S(1)} fusion(f32[4096,32]{1,0:T(8,128)} %gather_fusion.1, pred[4096]{0:T(1024)(128)(4,1)S(1)} %compare_and_fusion.5), kind=kLoop, calls=%fused_computation.4.clone.1 | loop fusion | flops 131072 | bytes 1052672 | tf_op jit(solution)/shard_map/while/body/eval_jaxpr/jvp(jit(_take))/select_n | solution.py:36
  197.0 0.9 copy.125
  197.9 0.9 copy.127
  199.5 14.1 %gather_fusion = f32[4096,32]{1,0:T(8,128)} fusion(f32[32,512]{0,1:T(8,128)S(1)} %copy.120, s32[4096]{0:T(1024)S(1)} %get-tuple-element.578), kind=kCustom, calls=%fused_computation.clone.clone.1 | custom fusion | bytes 1064960 | tf_op jit(solution)/shard_map/while/body/eval_jaxpr/jvp(jit(_take))/gather | solution.py:39
  213.6 3.6 %select_bitcast_fusion.4 = f32[32,4096]{0,1:T(8,128)S(1)} fusion(f32[4096,32]{1,0:T(8,128)} %gather_fusion, pred[4096]{0:T(1024)(128)(4,1)S(1)} %compare_and_fusion.4), kind=kLoop, calls=%fused_computation.5.clone.1 | loop fusion | flops 131072 | bytes 1052672 | tf_op jit(solution)/shard_map/while/body/eval_jaxpr/jvp(jit(_take))/select_n | solution.py:39
  218.9 0.6 multiply_reduce_fusion.24
  219.7 0.6 multiply_reduce_fusion.25
  220.9 1.3 multiply_reduce_fusion.26
  222.4 0.6 multiply_reduce_fusion.27
  223.8 1.0 fusion.36
  224.8 0.6 collective-permute-start.1
  225.4 6.7 %collective-permute-done.1 = f32[3,32,512]{2,1,0:T(8,128)S(1)} collective-permute-done((f32[3,32,512]{2,1,0:T(8,128)S(1)}, f32[3,32,512]{2,1,0:T(8,128)S(1)}, u32[]{:S(2)}, u32[]{:S(2)}) %collective-permute-start.1) | collective-permute-done | bytes 196640 | tf_op jit(solution)/shard_map/while/body/eval_jaxpr/ppermute | solution.py:16
  232.2 1.0 fusion.37
  233.1 0.9 collective-permute-start.2
  234.8 2.0 copy.133
  238.3 22.7 %scatter_custom_fusion.8 = f32[32,512]{0,1:T(8,128)S(1)} fusion(s32[4096]{0:T(1024)} %get-tuple-element.603, f32[4096,32]{1,0:T(8,128)} %copy.133, f32[]{:T(128)} %constant.70.clone.25..sunk), kind=kCustom, calls=%fused_computation.50.clone.1 | custom fusion | flops 131072 | bytes 66048 | tf_op jit(solution)/shard_map/while/body/eval_jaxpr/transpose(jvp(jit(_take)))/scatter-add | solution.py:36
  261.0 2.7 collective-permute-start.3
  263.8 4.4 %collective-permute-done.3 = f32[3,32,512]{2,1,0:T(8,128)S(1)} collective-permute-done((f32[3,32,512]{2,1,0:T(8,128)S(1)}, f32[3,32,512]{2,1,0:T(8,128)S(1)}, u32[]{:S(2)}, u32[]{:S(2)}) %collective-permute-start.3) | collective-permute-done | bytes 196640 | tf_op jit(solution)/shard_map/while/body/eval_jaxpr/ppermute | solution.py:16
  268.2 2.5 collective-permute-start.4
  270.8 7.0 %collective-permute-done.4 = f32[3,32,512]{2,1,0:T(8,128)S(1)} collective-permute-done((f32[3,32,512]{2,1,0:T(8,128)S(1)}, f32[3,32,512]{2,1,0:T(8,128)S(1)}, u32[]{:S(2)}, u32[]{:S(2)}) %collective-permute-start.4) | collective-permute-done | bytes 196640 | tf_op jit(solution)/shard_map/while/body/eval_jaxpr/ppermute | solution.py:16
  278.0 1.6 add_add_fusion.2
  279.7 22.5 %scatter_fusion = f32[32,512]{0,1:T(8,128)S(1)} fusion(f32[32,512]{0,1:T(8,128)S(1)} %copy.121, s32[4096]{0:T(1024)S(1)} %get-tuple-element.577, f32[4096,32]{1,0:T(8,128)S(1)} %copy.131), kind=kCustom, calls=%fused_computation.2.clone.1 | custom fusion | flops 131072 | bytes 1589248 | tf_op jit(solution)/shard_map/while/body/eval_jaxpr/transpose(jvp(jit(_take)))/scatter-add | solution.py:39
  302.2 0.7 copy.134
  302.9 0.7 fusion.42
  303.6 1.5 copy.104
  (155 shorter events, 16.8 us)
Async XLA Ops:
  46.4 0.7 copy-start
  47.1 47.5 %collective-permute-start = (f32[3,32,512]{2,1,0:T(8,128)}, f32[3,32,512]{2,1,0:T(8,128)}, u32[]{:S(2)}, u32[]{:S(2)}) collective-permute-start(f32[3,32,512]{2,1,0:T(8,128)} %pad_maximum_fusion.2), channel_id=1, source_target_pairs={{0,1},{1,0},{2,3},{3,2},{4,5},{5,4},{6,7},{7,6},{8,9},{9,8},{10,11... | collective-permute-start | bytes 589832 | tf_op jit(solution)/shard_map/while/body/eval_jaxpr/ppermute | solution.py:16
  67.9 2.1 copy-start.4
  89.0 0.8 copy-start.5
  89.0 1.0 copy-start.2
  89.1 1.1 copy-start.3
  94.2 0.8 copy-start.1
  96.0 7.9 %collective-permute-start.1 = (f32[3,32,512]{2,1,0:T(8,128)S(1)}, f32[3,32,512]{2,1,0:T(8,128)S(1)}, u32[]{:S(2)}, u32[]{:S(2)}) collective-permute-start(f32[3,32,512]{2,1,0:T(8,128)S(1)} %fusion.36), channel_id=1, source_target_pairs={{0,2},{1,3},{2,0},{3,1},{4,6},{5,7},{6,4},{7,5},{8,10},{9,11},{10,... | collective-permute-start | bytes 589832 | tf_op jit(solution)/shard_map/while/body/eval_jaxpr/ppermute | solution.py:16
  104.9 28.8 %collective-permute-start.2 = (f32[3,32,512]{2,1,0:T(8,128)S(1)}, f32[3,32,512]{2,1,0:T(8,128)S(1)}, u32[]{:S(2)}, u32[]{:S(2)}) collective-permute-start(f32[3,32,512]{2,1,0:T(8,128)S(1)} %fusion.37), channel_id=1, source_target_pairs={{0,4},{1,5},{2,6},{3,7},{4,0},{5,1},{6,2},{7,3},{8,12},{9,13},{10,... | collective-permute-start | bytes 589832 | tf_op jit(solution)/shard_map/while/body/eval_jaxpr/ppermute | solution.py:16
  109.9 24.4 %copy-start.6 = (f32[1,512]{1,0:T(1,128)S(1)}, f32[1,512]{1,0:T(1,128)}, u32[]{:S(2)}) copy-start(f32[1,512]{1,0:T(1,128)} %get-tuple-element.662) | copy-start | bytes 6148 | tf_op jit(solution)/shard_map/while
  110.3 31.1 %copy-start.13 = (f32[1,512]{1,0:T(1,128)S(1)}, f32[1,512]{1,0:T(1,128)}, u32[]{:S(2)}) copy-start(f32[1,512]{1,0:T(1,128)} %get-tuple-element.668) | copy-start | bytes 6148 | tf_op jit(solution)/shard_map/while
  110.3 38.1 %copy-start.7 = (f32[1,512]{1,0:T(1,128)S(1)}, f32[1,512]{1,0:T(1,128)}, u32[]{:S(2)}) copy-start(f32[1,512]{1,0:T(1,128)} %get-tuple-element.667) | copy-start | bytes 6148 | tf_op jit(solution)/shard_map/while
  110.3 38.1 %copy-start.8 = (f32[1,512]{1,0:T(1,128)S(1)}, f32[1,512]{1,0:T(1,128)}, u32[]{:S(2)}) copy-start(f32[1,512]{1,0:T(1,128)} %get-tuple-element.666) | copy-start | bytes 6148 | tf_op jit(solution)/shard_map/while
  110.3 38.1 %copy-start.9 = (f32[1,512]{1,0:T(1,128)S(1)}, f32[1,512]{1,0:T(1,128)}, u32[]{:S(2)}) copy-start(f32[1,512]{1,0:T(1,128)} %get-tuple-element.663) | copy-start | bytes 6148 | tf_op jit(solution)/shard_map/while
  110.4 38.1 %copy-start.10 = (f32[1,512]{1,0:T(1,128)S(1)}, f32[1,512]{1,0:T(1,128)}, u32[]{:S(2)}) copy-start(f32[1,512]{1,0:T(1,128)} %get-tuple-element.671) | copy-start | bytes 6148 | tf_op jit(solution)/shard_map/while
  110.4 38.1 %copy-start.11 = (f32[1,512]{1,0:T(1,128)S(1)}, f32[1,512]{1,0:T(1,128)}, u32[]{:S(2)}) copy-start(f32[1,512]{1,0:T(1,128)} %get-tuple-element.670) | copy-start | bytes 6148 | tf_op jit(solution)/shard_map/while
  110.4 38.1 %copy-start.12 = (f32[1,512]{1,0:T(1,128)S(1)}, f32[1,512]{1,0:T(1,128)}, u32[]{:S(2)}) copy-start(f32[1,512]{1,0:T(1,128)} %get-tuple-element.669) | copy-start | bytes 6148 | tf_op jit(solution)/shard_map/while
  133.8 6.2 %collective-permute-start.3 = (f32[3,32,512]{2,1,0:T(8,128)S(1)}, f32[3,32,512]{2,1,0:T(8,128)S(1)}, u32[]{:S(2)}, u32[]{:S(2)}) collective-permute-start(f32[3,32,512]{2,1,0:T(8,128)S(1)} %add.313), channel_id=1, source_target_pairs={{0,8},{1,9},{2,10},{3,11},{4,12},{5,13},{6,14},{7,15},{8,0},{9,1},... | collective-permute-start | bytes 589832 | tf_op jit(solution)/shard_map/while/body/eval_jaxpr/ppermute | solution.py:16
  140.0 8.4 %collective-permute-start.4 = (f32[3,32,512]{2,1,0:T(8,128)S(1)}, f32[3,32,512]{2,1,0:T(8,128)S(1)}, u32[]{:S(2)}, u32[]{:S(2)}) collective-permute-start(f32[3,32,512]{2,1,0:T(8,128)S(1)} %add.314), channel_id=1, source_target_pairs={{0,16},{1,17},{2,18},{3,19},{4,20},{5,21},{6,22},{7,23},{8,24},{9,... | collective-permute-start | bytes 589832 | tf_op jit(solution)/shard_map/while/body/eval_jaxpr/ppermute | solution.py:16
  175.2 0.7 copy-start
  175.9 47.5 %collective-permute-start = (f32[3,32,512]{2,1,0:T(8,128)}, f32[3,32,512]{2,1,0:T(8,128)}, u32[]{:S(2)}, u32[]{:S(2)}) collective-permute-start(f32[3,32,512]{2,1,0:T(8,128)} %pad_maximum_fusion.2), channel_id=1, source_target_pairs={{0,1},{1,0},{2,3},{3,2},{4,5},{5,4},{6,7},{7,6},{8,9},{9,8},{10,11... | collective-permute-start | bytes 589832 | tf_op jit(solution)/shard_map/while/body/eval_jaxpr/ppermute | solution.py:16
  196.6 2.1 copy-start.4
  217.8 0.8 copy-start.5
  217.8 1.0 copy-start.2
  217.8 1.1 copy-start.3
  223.0 0.8 copy-start.1
  224.8 7.4 %collective-permute-start.1 = (f32[3,32,512]{2,1,0:T(8,128)S(1)}, f32[3,32,512]{2,1,0:T(8,128)S(1)}, u32[]{:S(2)}, u32[]{:S(2)}) collective-permute-start(f32[3,32,512]{2,1,0:T(8,128)S(1)} %fusion.36), channel_id=1, source_target_pairs={{0,2},{1,3},{2,0},{3,1},{4,6},{5,7},{6,4},{7,5},{8,10},{9,11},{10,... | collective-permute-start | bytes 589832 | tf_op jit(solution)/shard_map/while/body/eval_jaxpr/ppermute | solution.py:16
  233.1 27.9 %collective-permute-start.2 = (f32[3,32,512]{2,1,0:T(8,128)S(1)}, f32[3,32,512]{2,1,0:T(8,128)S(1)}, u32[]{:S(2)}, u32[]{:S(2)}) collective-permute-start(f32[3,32,512]{2,1,0:T(8,128)S(1)} %fusion.37), channel_id=1, source_target_pairs={{0,4},{1,5},{2,6},{3,7},{4,0},{5,1},{6,2},{7,3},{8,12},{9,13},{10,... | collective-permute-start | bytes 589832 | tf_op jit(solution)/shard_map/while/body/eval_jaxpr/ppermute | solution.py:16
  237.2 26.5 %copy-start.6 = (f32[1,512]{1,0:T(1,128)S(1)}, f32[1,512]{1,0:T(1,128)}, u32[]{:S(2)}) copy-start(f32[1,512]{1,0:T(1,128)} %get-tuple-element.662) | copy-start | bytes 6148 | tf_op jit(solution)/shard_map/while
  237.6 33.2 %copy-start.13 = (f32[1,512]{1,0:T(1,128)S(1)}, f32[1,512]{1,0:T(1,128)}, u32[]{:S(2)}) copy-start(f32[1,512]{1,0:T(1,128)} %get-tuple-element.668) | copy-start | bytes 6148 | tf_op jit(solution)/shard_map/while
  237.6 40.2 %copy-start.7 = (f32[1,512]{1,0:T(1,128)S(1)}, f32[1,512]{1,0:T(1,128)}, u32[]{:S(2)}) copy-start(f32[1,512]{1,0:T(1,128)} %get-tuple-element.667) | copy-start | bytes 6148 | tf_op jit(solution)/shard_map/while
  237.6 40.2 %copy-start.8 = (f32[1,512]{1,0:T(1,128)S(1)}, f32[1,512]{1,0:T(1,128)}, u32[]{:S(2)}) copy-start(f32[1,512]{1,0:T(1,128)} %get-tuple-element.666) | copy-start | bytes 6148 | tf_op jit(solution)/shard_map/while
  237.6 40.2 %copy-start.9 = (f32[1,512]{1,0:T(1,128)S(1)}, f32[1,512]{1,0:T(1,128)}, u32[]{:S(2)}) copy-start(f32[1,512]{1,0:T(1,128)} %get-tuple-element.663) | copy-start | bytes 6148 | tf_op jit(solution)/shard_map/while
  237.6 40.2 %copy-start.10 = (f32[1,512]{1,0:T(1,128)S(1)}, f32[1,512]{1,0:T(1,128)}, u32[]{:S(2)}) copy-start(f32[1,512]{1,0:T(1,128)} %get-tuple-element.671) | copy-start | bytes 6148 | tf_op jit(solution)/shard_map/while
  237.6 40.2 %copy-start.11 = (f32[1,512]{1,0:T(1,128)S(1)}, f32[1,512]{1,0:T(1,128)}, u32[]{:S(2)}) copy-start(f32[1,512]{1,0:T(1,128)} %get-tuple-element.670) | copy-start | bytes 6148 | tf_op jit(solution)/shard_map/while
  237.7 40.2 %copy-start.12 = (f32[1,512]{1,0:T(1,128)S(1)}, f32[1,512]{1,0:T(1,128)}, u32[]{:S(2)}) copy-start(f32[1,512]{1,0:T(1,128)} %get-tuple-element.669) | copy-start | bytes 6148 | tf_op jit(solution)/shard_map/while
  261.0 7.1 %collective-permute-start.3 = (f32[3,32,512]{2,1,0:T(8,128)S(1)}, f32[3,32,512]{2,1,0:T(8,128)S(1)}, u32[]{:S(2)}, u32[]{:S(2)}) collective-permute-start(f32[3,32,512]{2,1,0:T(8,128)S(1)} %add.313), channel_id=1, source_target_pairs={{0,8},{1,9},{2,10},{3,11},{4,12},{5,13},{6,14},{7,15},{8,0},{9,1},... | collective-permute-start | bytes 589832 | tf_op jit(solution)/shard_map/while/body/eval_jaxpr/ppermute | solution.py:16
  268.2 9.6 %collective-permute-start.4 = (f32[3,32,512]{2,1,0:T(8,128)S(1)}, f32[3,32,512]{2,1,0:T(8,128)S(1)}, u32[]{:S(2)}, u32[]{:S(2)}) collective-permute-start(f32[3,32,512]{2,1,0:T(8,128)S(1)} %add.314), channel_id=1, source_target_pairs={{0,16},{1,17},{2,18},{3,19},{4,20},{5,21},{6,22},{7,23},{8,24},{9,... | collective-permute-start | bytes 589832 | tf_op jit(solution)/shard_map/while/body/eval_jaxpr/ppermute | solution.py:16
